TPU v7x, 256 devices: a whole 4x4x8 slice. The times are simulated.
256 devices in a mesh: ep: 8 (over y, core), fsdp: 32 (over z, x).
Axes of the slice: x: 4, y: 4, z: 8, core: 2. Of those that a mesh axis runs over, the one named last changes fastest.
Arguments:
- w_down: float32 [16, 6400, 4096], P('ep', None, 'fsdp'), may hold values from -0.15625 to 0.15625
- router_weight: float32 [4096, 16], P('fsdp', 'ep'), may hold values from -0.09375 to 0.09375
- router_gain: float32 [4096], P('fsdp'), may hold values from 0.25 to 1.75
Outputs:
- serve_down: bfloat16 [16, 6400, 4096], P('ep', 'fsdp')
- scale_down: float32 [16, 6400], P('ep', 'fsdp')
- serve_router: bfloat16 [4096, 16], replicated
All inputs are finite; a program needn't handle non-finite values.
Results may differ from a plain program's by a relative error of at most 0.001.
Values may be sent and summed in bfloat16 or wider, within the bound.
A program may use at most 64 MiB of HBM per device.

v0:
```python
import jax
import jax.numpy as jnp
from jax import lax
from jax.sharding import Mesh
from jax.sharding import PartitionSpec as P

FSDP = ("fsdp_0", "fsdp_1")


def by_axis(array, axes):
    for axis in axes:
        array = lax.psum(array, axis)
    return array


def in_order(parts, dim):
    lengths = list(parts.shape[1:])
    lengths[dim] *= parts.shape[0]
    return jnp.moveaxis(parts, 0, dim).reshape(lengths)


def copy_for_each(array, axis):
    size = lax.axis_size(axis)
    return lax.all_to_all(
        jnp.broadcast_to(array[None], (size, *array.shape)), axis, 0, 0, tiled=True
    )


def gather_directly(array, axis, dim):
    return in_order(copy_for_each(array, axis), dim)


def body(w_down, router_weight, router_gain):
    total_down = by_axis(jnp.sum(w_down * w_down, axis=2), FSDP)
    scale_down = jnp.sqrt(total_down)
    narrow_down = (w_down / jnp.expand_dims(scale_down, 2)).astype(jnp.bfloat16)
    serve_down = lax.all_to_all(narrow_down, FSDP, split_axis=1, concat_axis=2, tiled=True)
    scale_down = lax.dynamic_slice_in_dim(
        scale_down, lax.axis_index(FSDP) * serve_down.shape[1], serve_down.shape[1], axis=1
    )
    part_router = (router_weight * router_gain[:, None]).astype(jnp.bfloat16)
    row_router = gather_directly(part_router, FSDP, 0)
    serve_router = lax.all_gather(row_router, "ep", axis=1, tiled=True)
    return (serve_down, scale_down, serve_router)


def solution(mesh):
    split = Mesh(mesh.devices.reshape(mesh.shape["ep"], 8, 4), ("ep", "fsdp_0", "fsdp_1"))
    return jax.shard_map(
        body,
        mesh=split,
        in_specs=(P("ep", None, FSDP), P(FSDP, "ep"), P(FSDP)),
        out_specs=(P("ep", FSDP, None), P("ep", FSDP), P()),
        check_vma=False,
    )
```

profile of v0, /device:TPU:8, one launch (start us, length us, event | category | flops | bytes accessed | tf_op | source)
XLA Modules:
  0.0 177.8 jit_solution(15432574918795712005)
XLA Ops:
  0.6 0.7 multiply_convert_fusion
  1.3 0.6 broadcast_in_dim.2
  1.9 11.3 %all-to-all-start.1 = ((bf16[32,128,2]{1,2,0:T(2,128)(2,1)}), bf16[32,128,2]{1,2,0:T(2,128)(2,1)S(1)}, u32[]{:S(2)}, u32[]{:S(2)}) async-start(bf16[32,128,2]{1,2,0:T(2,128)(2,1)} %broadcast_in_dim.2), calls=%async_computation.1 | async-start | bytes 32768 | tf_op jit(solution)/shard_map/all_to_all | solution.py:24
  13.3 4.6 %multiply_reduce_fusion = f32[2,6400]{1,0:T(2,128)S(1)} fusion(f32[2,6400,128]{2,1,0:T(8,128)} %param.3), kind=kLoop, calls=%fused_computation.1 | loop fusion | flops 3264000 | bytes 6604800 | tf_op jit(solution)/shard_map/reduce_sum | solution.py:34
  17.9 30.5 %psum.14 = f32[2,6400]{1,0:T(2,128)S(1)} all-reduce(f32[2,6400]{1,0:T(2,128)S(1)} %multiply_reduce_fusion), channel_id=1, replica_groups=mesh['ep'=8,'fsdp_0'=8,'fsdp_1'=4] {'fsdp_0'}, use_global_device_ids=true, to_apply=%region_1.0 | all-reduce | flops 12800 | bytes 102400 | tf_op jit(solution)/shard_map/psum | solution.py:12
  48.4 17.4 %psum.15 = f32[2,6400]{1,0:T(2,128)S(1)} all-reduce(f32[2,6400]{1,0:T(2,128)S(1)} %psum.14), channel_id=1, replica_groups=mesh['ep'=8,'fsdp_0'=8,'fsdp_1'=4] {'fsdp_1'}, use_global_device_ids=true, to_apply=%region_2.0 | all-reduce | flops 12800 | bytes 102400 | tf_op jit(solution)/shard_map/psum | solution.py:12
  65.8 0.1 sqrt.3
  65.9 4.7 %divide_convert_fusion = bf16[2,6400,128]{2,1,0:T(8,128)(2,1)S(1)} fusion(f32[2,6400,128]{2,1,0:T(8,128)} %param.3, f32[2,6400]{1,0:T(2,128)S(1)} %sqrt.3), kind=kLoop, calls=%fused_computation | loop fusion | flops 3276800 | bytes 9881600 | tf_op jit(solution)/shard_map/convert_element_type | solution.py:36
  70.6 27.9 %copy.10 = bf16[2,6400,128]{2,0,1:T(2,128)(2,1)} copy(bf16[2,6400,128]{2,1,0:T(8,128)(2,1)S(1)} %divide_convert_fusion) | data formatting | bytes 6553600 | tf_op jit(solution)/shard_map/convert_element_type | solution.py:36
  98.5 0.0 all-to-all-done.1
  98.5 5.7 %all-to-all-start = ((bf16[2,6400,128]{2,0,1:T(2,128)(2,1)}), bf16[2,6400,128]{2,0,1:T(2,128)(2,1)S(1)}, u32[]{:S(2)}, u32[]{:S(2)}) async-start(bf16[2,6400,128]{2,0,1:T(2,128)(2,1)} %copy.10), calls=%async_computation | async-start | bytes 6553600 | tf_op jit(solution)/shard_map/all_to_all | solution.py:37
  104.2 0.7 constant_dynamic-slice_fusion
  104.9 12.9 %all-gather = bf16[8,2,4096]{2,1,0:T(2,128)(2,1)S(1)} all-gather(bf16[1,2,4096]{2,1,0:T(2,128)(2,1)S(1)} %bitcast.13), channel_id=1, replica_groups=mesh['ep'=8,'fsdp_0'=8,'fsdp_1'=4] {'ep'}, dimensions={0}, use_global_device_ids=true | all-gather | bytes 147456 | tf_op jit(solution)/shard_map/all_gather | solution.py:43
  117.8 0.7 reshape.14
  118.5 50.5 %all-to-all-done = bf16[2,6400,128]{2,0,1:T(2,128)(2,1)S(1)} async-done(((bf16[2,6400,128]{2,0,1:T(2,128)(2,1)}), bf16[2,6400,128]{2,0,1:T(2,128)(2,1)S(1)}, u32[]{:S(2)}, u32[]{:S(2)}) %all-to-all-start) | async-done | bytes 3276832 | tf_op jit(solution)/shard_map/all_to_all | solution.py:37
  169.1 2.5 %copy.11 = bf16[2,200,32,128]{3,2,1,0:T(8,128)(2,1)} copy(bf16[2,200,32,128]{3,0,1,2:T(2,128)(2,1)S(1)} %bitcast.11) | data formatting | bytes 6553600 | tf_op jit(solution)/shard_map/all_to_all | solution.py:37
  171.6 6.2 %all_to_all.19 = bf16[2,200,4096]{2,1,0:T(8,128)(2,1)} reshape(bf16[2,200,32,128]{3,2,1,0:T(8,128)(2,1)} %copy.11) | data formatting | bytes 6553600 | tf_op jit(solution)/shard_map/all_to_all | solution.py:37
Async XLA Ops:
  1.9 96.6 %all-to-all-start.1 = ((bf16[32,128,2]{1,2,0:T(2,128)(2,1)}), bf16[32,128,2]{1,2,0:T(2,128)(2,1)S(1)}, u32[]{:S(2)}, u32[]{:S(2)}) async-start(bf16[32,128,2]{1,2,0:T(2,128)(2,1)} %broadcast_in_dim.2), calls=%async_computation.1 | async-start | bytes 32768 | tf_op jit(solution)/shard_map/all_to_all | solution.py:24
  98.5 70.6 %all-to-all-start = ((bf16[2,6400,128]{2,0,1:T(2,128)(2,1)}), bf16[2,6400,128]{2,0,1:T(2,128)(2,1)S(1)}, u32[]{:S(2)}, u32[]{:S(2)}) async-start(bf16[2,6400,128]{2,0,1:T(2,128)(2,1)} %copy.10), calls=%async_computation | async-start | bytes 6553600 | tf_op jit(solution)/shard_map/all_to_all | solution.py:37
where the time goes:
time: 178 us
  blocking collectives  60.9 us (34%)
  waiting for transfers between devices  50.5 us (28%)
  local copies, waits for them, and re-layouts  38.6 us (22%)
  starting transfers between devices  17 us (10%)
  other arithmetic  10 us (6%)
    all_to_all x1, waiting for transfers between devices, body(): lax.all_to_all(narrow_down, FSDP, split_axis=1, concat_axis=2, tiled=True)  50.5 us
    psum x2, blocking collectives, by_axis(): array = lax.psum(array, axis)  47.9 us
    convert_element_type x1, local copies, waits for them, and re-layouts, body(): narrow_down = (w_down / jnp.expand_dims(scale_down, 2)).astype(jnp.bfloat16)  27.9 us
    all_gather x1, blocking collectives, body(): serve_router = lax.all_gather(row_router, 'ep', axis=1, tiled=True)  12.9 us
    all_to_all x1, starting transfers between devices, copy_for_each(): lax.all_to_all(jnp.broadcast_to(array[None], (size, *array.shape)), axis,...  11.3 us
    all_to_all x2, local copies, waits for them, and re-layouts, body(): lax.all_to_all(narrow_down, FSDP, split_axis=1, concat_axis=2, tiled=True)  8.73 us
    all_to_all x1, starting transfers between devices, body(): lax.all_to_all(narrow_down, FSDP, split_axis=1, concat_axis=2, tiled=True)  5.7 us
    convert_element_type x1, other arithmetic, body(): narrow_down = (w_down / jnp.expand_dims(scale_down, 2)).astype(jnp.bfloat16)  4.71 us
  transfers between devices with their start and end apart: 2, of which 1 were waited for; matrix products, arithmetic and copies ran while one was open for 22% of the time, Pallas kernels for 0%

commit v1 on v0

v1 whole, which is shorter than its diff:
```python
import functools

import jax
import jax.numpy as jnp
from jax import lax
from jax.experimental import pallas as pl
from jax.experimental.pallas import tpu as pltpu
from jax.sharding import PartitionSpec as P

MESH = pl.DeviceIdType.MESH
F32, BF16 = jnp.float32, jnp.bfloat16
CHUNKS = 4


def peer(k, z, x):
    j, dx = k // 4, lax.rem(k, 4)
    odd = lax.rem(j, 2)
    dz = odd * ((j + 1) // 2) + (1 - odd) * (8 - j // 2)
    return lax.rem(z + dz, 8) * 4 + lax.rem(x + dx, 4)


def row_sums(block):
    square = block * block
    high = square.astype(BF16)
    rest = square - high.astype(F32)
    middle = rest.astype(BF16)
    low = (rest - middle.astype(F32)).astype(BF16)
    ones = jnp.ones((8, 128), BF16)
    dot = lambda part: lax.dot_general(
        ones, part, (((1,), (1,)), ((), ())), preferred_element_type=F32
    )
    return (dot(high) + dot(middle) + dot(low))[:1]


def kernel(
    w_ref, router_ref, gain_ref, down_ref, scale_ref, serve_router_ref,
    w, part, landed, total, scales, send, rows, columns,
    load_sem, part_send, part_recv, scale_send, scale_recv,
    down_send, down_recv, router_send, router_recv,
):
    n, width = 32, 200
    ep, me = lax.axis_index("ep"), lax.axis_index("fsdp")
    z, x = me // 4, lax.rem(me, 4)

    span = 6400 // CHUNKS
    loads = [
        pltpu.make_async_copy(
            w_ref.at[:, pl.ds(c * span, span), :], w.at[:, pl.ds(c * span, span), :], load_sem.at[c]
        )
        for c in range(CHUNKS)
    ]
    for load in loads:
        load.start()

    barrier = pltpu.get_barrier_semaphore()

    @pl.loop(1, n)
    def _(k):
        pl.semaphore_signal(barrier, inc=1, device_id={"fsdp": peer(k, z, x)}, device_id_type=MESH)

    @pl.loop(1, 8)
    def _(k):
        pl.semaphore_signal(barrier, inc=1, device_id={"ep": lax.rem(ep + k, 8)}, device_id_type=MESH)

    router = router_ref[...] * gain_ref[...]

    for c in range(CHUNKS):
        loads[c].wait()

        @pl.loop(c * (n // CHUNKS), (c + 1) * (n // CHUNKS))
        def _(t):
            block = w[:, pl.ds(pl.multiple_of(t * width, 8), width), :].reshape(2 * width, 128)
            part[t, :, 0:400] = row_sums(block)
            part[t, :, 512:640] = router[0:1]
            part[t, :, 640:768] = router[1:2]

    pl.semaphore_wait(barrier, 38)

    @pl.loop(1, n)
    def _(k):
        t = peer(k, z, x)
        pltpu.make_async_remote_copy(
            src_ref=part.at[t], dst_ref=landed.at[me], send_sem=part_send, recv_sem=part_recv,
            device_id={"fsdp": t}, device_id_type=MESH,
        ).start()

    landed[me] = part[me]
    pltpu.make_async_copy(landed.at[pl.ds(0, n - 1)], landed.at[pl.ds(0, n - 1)], part_recv).wait()
    scale = jnp.sqrt(jnp.sum(landed[:, :, 0:512], axis=0))
    total[...] = scale
    scales[me] = scale
    scale_ref[0:1] = scale[:, 0:width]
    scale_ref[1:2] = scale[:, width : 2 * width]

    @pl.loop(0, n)
    def _(s):
        lanes = pl.ds(pl.multiple_of(s * 128, 128), 128)
        rows[0:1, lanes] = landed[s, :, 512:640]
        rows[1:2, lanes] = landed[s, :, 640:768]

    @pl.loop(1, n)
    def _(k):
        t = peer(k, z, x)
        pltpu.make_async_remote_copy(
            src_ref=total, dst_ref=scales.at[me], send_sem=scale_send, recv_sem=scale_recv,
            device_id={"fsdp": t}, device_id_type=MESH,
        ).start()

    @pl.loop(1, 8)
    def _(k):
        pltpu.make_async_remote_copy(
            src_ref=rows, dst_ref=columns.at[ep], send_sem=router_send, recv_sem=router_recv,
            device_id={"ep": lax.rem(ep + k, 8)}, device_id_type=MESH,
        ).start()

    columns[ep] = rows[...]
    pltpu.make_async_copy(scales.at[pl.ds(0, n - 1)], scales.at[pl.ds(0, n - 1)], scale_recv).wait()

    def scaled(t):
        inverse = 1.0 / scales[t][:, 0:400]
        block = w[:, pl.ds(pl.multiple_of(t * width, 8), width), :].reshape(2 * width, 128)
        return (block * jnp.broadcast_to(inverse, (128, 400)).T).astype(BF16)

    lanes = pl.ds(pl.multiple_of(me * 128, 128), 128)

    def go(k):
        t = peer(k, z, x)
        pltpu.make_async_remote_copy(
            src_ref=send.at[t], dst_ref=down_ref.at[:, :, lanes], send_sem=down_send, recv_sem=down_recv,
            device_id={"fsdp": t}, device_id_type=MESH,
        ).start()

    @pl.loop(1, n)
    def _(k):
        t = peer(k, z, x)
        value = scaled(t)
        send[t, 0] = value[0:width]
        send[t, 1] = value[width:]

        @pl.when(k > 1)
        def _():
            go(k - 1)

    own = scaled(me)
    down_ref[0, :, lanes] = own[0:width]
    down_ref[1, :, lanes] = own[width:]
    go(n - 1)

    pltpu.make_async_copy(columns.at[pl.ds(0, 7)], columns.at[pl.ds(0, 7)], router_recv).wait()
    for e in range(8):
        serve_router_ref[2 * e : 2 * e + 2, :] = columns[e].astype(BF16)

    pltpu.make_async_copy(part.at[pl.ds(0, n - 1)], part.at[pl.ds(0, n - 1)], part_send).wait()
    pltpu.make_async_copy(scales.at[pl.ds(0, n - 1)], scales.at[pl.ds(0, n - 1)], scale_send).wait()
    pltpu.make_async_copy(columns.at[pl.ds(0, 7)], columns.at[pl.ds(0, 7)], router_send).wait()
    pltpu.make_async_copy(send.at[pl.ds(0, n - 1)], send.at[pl.ds(0, n - 1)], down_send).wait()
    pltpu.make_async_copy(send.at[pl.ds(0, n - 1)], send.at[pl.ds(0, n - 1)], down_recv).wait()


def body(w_down, router_weight, router_gain):
    vmem, hbm = pl.BlockSpec(memory_space=pltpu.VMEM), pl.BlockSpec(memory_space=pltpu.HBM)
    dma = pltpu.SemaphoreType.DMA
    down, scale, router = pl.pallas_call(
        kernel,
        out_shape=(
            jax.ShapeDtypeStruct((2, 200, 4096), BF16),
            jax.ShapeDtypeStruct((2, 200), F32),
            jax.ShapeDtypeStruct((16, 4096), BF16),
        ),
        in_specs=[hbm, vmem, vmem],
        out_specs=(vmem, vmem, vmem),
        scratch_shapes=[
            pltpu.VMEM((2, 6400, 128), F32),
            pltpu.VMEM((32, 1, 768), F32),
            pltpu.VMEM((32, 1, 768), F32),
            pltpu.VMEM((1, 512), F32),
            pltpu.VMEM((32, 1, 512), F32),
            pltpu.VMEM((32, 2, 200, 128), BF16),
            pltpu.VMEM((2, 4096), F32),
            pltpu.VMEM((8, 2, 4096), F32),
            dma((CHUNKS,)), dma, dma, dma, dma, dma, dma, dma, dma,
        ],
        compiler_params=pltpu.CompilerParams(
            collective_id=0, has_side_effects=True, vmem_limit_bytes=62_000_000
        ),
        name="serve",
    )(w_down, router_weight.T, router_gain[None])
    return down, scale, router.T


def solution(mesh):
    return jax.shard_map(
        body,
        mesh=mesh,
        in_specs=(P("ep", None, "fsdp"), P("fsdp", "ep"), P("fsdp")),
        out_specs=(P("ep", "fsdp", None), P("ep", "fsdp"), P()),
        check_vma=False,
    )
```

time: 178 us -> 111 us (0.62)
  the two profiles are of different devices: /device:TPU:8 before, /device:TPU:32 now
where the time goes in v1:
time: 111 us; the launch traced here: 109 us
  Pallas kernels  103 us (93%)
  local copies, waits for them, and re-layouts  5.28 us (5%)
    pallas_call x1, Pallas kernels, body(): pl.pallas_call(kernel, out_shape=(jax.ShapeDtypeStruct((2, 200, 4096), BF...  103 us
    unnamed x7, local copies, waits for them, and re-layouts  5.28 us

profile of v1, /device:TPU:32, one launch (start us, length us, event | category | flops | bytes accessed | tf_op | source)
XLA Modules:
  0.0 108.5 jit_solution(13473714547099673273)
XLA Ops:
  0.6 102.6 %serve.1 = (bf16[2,200,4096]{2,1,0:T(8,128)(2,1)}, f32[2,200]{1,0:T(2,128)}, bf16[16,4096]{1,0:T(8,128)(2,1)}) custom-call(f32[2,6400,128]{2,1,0:T(8,128)} %w_ref.1, f32[2,128]{1,0:T(2,128)} %bitcast.4, f32[1,128]{1,0:T(1,128)} %bitcast.5), custom_call_target="tpu_custom_call" | custom-call | tf_op jit(solution)/shard_map/serve/pallas_call | solution.py:163
  103.2 0.0 copy-start.1
  103.2 0.0 copy-start
  103.2 4.0 %copy.9 = bf16[2,200,4096]{2,1,0:T(8,128)(2,1)} copy(bf16[2,200,4096]{2,1,0:T(8,128)(2,1)} %get-tuple-element.12) | data formatting | bytes 6553600
  107.3 0.0 copy-done.1
  107.3 0.6 copy.10
  107.9 0.0 copy-done
  107.9 0.7 copy.11
Async XLA Ops:
  103.2 4.1 %copy-start.1 = (f32[2,200]{1,0:T(2,128)S(1)}, f32[2,200]{1,0:T(2,128)}, u32[]{:S(2)}) copy-start(f32[2,200]{1,0:T(2,128)} %get-tuple-element.13) | copy-start | bytes 4804
  103.2 4.6 %copy-start = (bf16[16,4096]{1,0:T(8,128)(2,1)S(1)}, bf16[16,4096]{1,0:T(8,128)(2,1)}, u32[]{:S(2)}) copy-start(bf16[16,4096]{1,0:T(8,128)(2,1)} %get-tuple-element.8) | copy-start | bytes 393220

commit v2 on v0

v2 whole, which is shorter than its diff:
```python
import jax
import jax.numpy as jnp
from jax import lax
from jax.experimental import pallas as pl
from jax.experimental.pallas import tpu as pltpu
from jax.sharding import PartitionSpec as P

MESH = pl.DeviceIdType.MESH
F32, BF16 = jnp.float32, jnp.bfloat16
Z, X, EP = 8, 4, 8
PARTNERS = Z * X
ROWS = 200
CHUNKS = 4
VMEM_LIMIT = 40_000_000

NEAR = sorted(
    ((dz, dx) for dz in range(Z) for dx in range(X) if dz or dx),
    key=lambda o: (min(o[0], Z - o[0]) + min(o[1], X - o[1]), o),
)


def stretches(z, x):
    def at(dz, dx):
        return lax.rem(z + dz, Z) * X + lax.rem(x + dx, X)

    def close(i):
        return at(1 + 6 * lax.rem(i, 2), i // 2)

    def wide(i):
        j = lax.rem(i, 6)
        odd = lax.rem(j, 2)
        return at((1 - odd) * (4 + j // 2) + odd * (4 - (j + 1) // 2 - j // 5), 3 - i // 6)

    return (8, close), (23, wide)


def row_sums(block):
    square = block * block
    total = jnp.broadcast_to(jnp.sum(square, axis=1, keepdims=True), square.shape)
    rows = lax.broadcasted_iota(jnp.int32, (128, 128), 0)
    own = rows == lax.broadcasted_iota(jnp.int32, (128, 128), 1)
    return jnp.concatenate(
        [
            jnp.sum(
                jnp.where(own[: min(128, 2 * ROWS - r)], total[r : r + 128], 0.0),
                axis=0,
                keepdims=True,
            )
            for r in range(0, 2 * ROWS, 128)
        ],
        axis=1,
    )


def serve(
    w_ref, weight_ref, gain_ref, down_ref, scale_ref, router_ref,
    w, weight, gain, part, landed, total, scales, send, rows, columns,
    load_sem, part_send, part_recv, scale_send, scale_recv,
    down_send, down_recv, router_send, router_recv,
):
    ep, me = lax.axis_index("ep"), lax.axis_index("fsdp")
    z, x = me // X, lax.rem(me, X)

    span = PARTNERS * ROWS // CHUNKS
    loads = []
    for c in range(CHUNKS):
        piece = pl.ds(c * span, span)
        loads.append((w_ref.at[:, piece, :], w.at[:, piece, :]))
    loads += [(weight_ref, weight), (gain_ref, gain)]
    loads = [pltpu.make_async_copy(*pair, load_sem.at[i]) for i, pair in enumerate(loads)]
    for load in loads:
        load.start()

    barrier = pltpu.get_barrier_semaphore()
    zs = [lax.rem(z + d, Z) * X for d in range(Z)]
    xs = [lax.rem(x + d, X) for d in range(X)]
    partners = [zs[dz] + xs[dx] for dz, dx in NEAR]
    peers = [lax.rem(ep + d, EP) for d in range(1, EP)]
    for t in reversed(partners):
        pl.semaphore_signal(barrier, inc=1, device_id={"fsdp": t}, device_id_type=MESH)
    for e in peers:
        pl.semaphore_signal(barrier, inc=1, device_id={"ep": e}, device_id_type=MESH)

    loads[CHUNKS].wait()
    loads[CHUNKS + 1].wait()
    router = weight[...] * gain[...]

    def rows_of(t):
        block = w[:, pl.ds(pl.multiple_of(t * ROWS, 8), ROWS), :]
        return block.reshape(2 * ROWS, 128)

    for c in range(CHUNKS):
        loads[c].wait()
        each = PARTNERS // CHUNKS

        @pl.loop(c * each, (c + 1) * each, unroll=each)
        def _(t):
            part[t, :, 0:512] = row_sums(rows_of(t))
            part[t, :, 512:640] = router[0:1]
            part[t, :, 640:768] = router[1:2]

    pl.semaphore_wait(barrier, len(partners) + len(peers))
    for t in reversed(partners):
        pltpu.make_async_remote_copy(
            src_ref=part.at[t], dst_ref=landed.at[me], send_sem=part_send, recv_sem=part_recv,
            device_id={"fsdp": t}, device_id_type=MESH,
        ).start()

    landed[me] = part[me]
    others = pl.ds(0, PARTNERS - 1)
    pltpu.make_async_copy(landed.at[others], landed.at[others], part_recv).wait()
    scale = jnp.sqrt(jnp.sum(landed[:, :, 0:512], axis=0))
    total[...] = scale
    scales[me] = scale
    for e in range(2):
        scale_ref[e : e + 1] = scale[:, e * ROWS : (e + 1) * ROWS]
    for t in partners:
        pltpu.make_async_remote_copy(
            src_ref=total, dst_ref=scales.at[me], send_sem=scale_send, recv_sem=scale_recv.at[me],
            device_id={"fsdp": t}, device_id_type=MESH,
        ).start()

    @pl.loop(0, PARTNERS)
    def _(s):
        lanes = pl.ds(pl.multiple_of(s * 128, 128), 128)
        rows[0:1, lanes] = landed[s, :, 512:640]
        rows[1:2, lanes] = landed[s, :, 640:768]

    columns[ep] = rows[...]
    for e in peers:
        pltpu.make_async_remote_copy(
            src_ref=rows, dst_ref=columns.at[ep], send_sem=router_send, recv_sem=router_recv,
            device_id={"ep": e}, device_id_type=MESH,
        ).start()

    lanes = pl.ds(pl.multiple_of(me * 128, 128), 128)

    def scaled(t):
        inverse = 1.0 / scales[t, :, 0 : 2 * ROWS]
        return (rows_of(t) * jnp.broadcast_to(inverse, (128, 2 * ROWS)).T).astype(BF16)

    def make(t):
        pltpu.make_async_copy(scales.at[t], scales.at[t], scale_recv.at[t]).wait()
        value = scaled(t)
        send[t, 0] = value[:ROWS]
        send[t, 1] = value[ROWS:]

    def go(t):
        pltpu.make_async_remote_copy(
            src_ref=send.at[t], dst_ref=down_ref.at[:, :, lanes], send_sem=down_send, recv_sem=down_recv,
            device_id={"fsdp": t}, device_id_type=MESH,
        ).start()

    for count, partner in stretches(z, x):
        make(partner(0))

        @pl.loop(1, count)
        def _(i):
            make(partner(i))
            go(partner(i - 1))

        go(partner(count - 1))

    own = scaled(me)
    down_ref[0, :, lanes] = own[:ROWS]
    down_ref[1, :, lanes] = own[ROWS:]

    pltpu.make_async_copy(columns.at[pl.ds(0, EP - 1)], columns.at[pl.ds(0, EP - 1)], router_recv).wait()
    for e in range(EP):
        router_ref[2 * e : 2 * e + 2, :] = columns[e].astype(BF16)

    pltpu.make_async_copy(part.at[others], part.at[others], part_send).wait()
    pltpu.make_async_copy(scales.at[others], scales.at[others], scale_send).wait()
    pltpu.make_async_copy(columns.at[pl.ds(0, EP - 1)], columns.at[pl.ds(0, EP - 1)], router_send).wait()
    pltpu.make_async_copy(send.at[others], send.at[others], down_send).wait()
    pltpu.make_async_copy(send.at[others], send.at[others], down_recv).wait()


def put_out(down_ref, scale_ref, router_ref, down_out, scale_out, router_out, sem):
    pairs = [(scale_ref, scale_out), (router_ref, router_out)]
    for e in range(2):
        for r in range(0, ROWS, 40):
            piece = pl.ds(r, 40)
            pairs.append((down_ref.at[e, piece], down_out.at[e, piece]))
    copies = [pltpu.make_async_copy(*pair, sem.at[i]) for i, pair in enumerate(pairs)]
    for copy in copies:
        copy.start()
    for copy in copies:
        copy.wait()


def body(w_down, router_weight, router_gain):
    vmem, hbm = pl.BlockSpec(memory_space=pltpu.VMEM), pl.BlockSpec(memory_space=pltpu.HBM)
    dma = pltpu.SemaphoreType.DMA
    outs = (
        jax.ShapeDtypeStruct((2, ROWS, PARTNERS * 128), BF16),
        jax.ShapeDtypeStruct((2, ROWS), F32),
        jax.ShapeDtypeStruct((2 * EP, PARTNERS * 128), BF16),
    )
    operands = (w_down, router_weight.T, router_gain[None])
    served = pl.pallas_call(
        serve,
        out_shape=outs,
        in_specs=[hbm] * 3,
        out_specs=(vmem,) * 3,
        scratch_shapes=[
            pltpu.VMEM((2, PARTNERS * ROWS, 128), F32),
            pltpu.VMEM((2, 128), F32),
            pltpu.VMEM((1, 128), F32),
            pltpu.VMEM((PARTNERS, 1, 768), F32),
            pltpu.VMEM((PARTNERS, 1, 768), F32),
            pltpu.VMEM((1, 512), F32),
            pltpu.VMEM((PARTNERS, 1, 512), F32),
            pltpu.VMEM((PARTNERS, 2, ROWS, 128), BF16),
            pltpu.VMEM((2, PARTNERS * 128), F32),
            pltpu.VMEM((EP, 2, PARTNERS * 128), F32),
            dma((CHUNKS + 2,)), dma, dma, dma, dma((PARTNERS,)), dma, dma, dma, dma,
        ],
        compiler_params=pltpu.CompilerParams(
            collective_id=0, has_side_effects=True, vmem_limit_bytes=VMEM_LIMIT
        ),
        name="serve",
    )(*(pltpu.with_memory_space_constraint(a, pltpu.HBM) for a in operands))
    down, scale, router = pl.pallas_call(
        put_out,
        out_shape=outs,
        in_specs=[vmem] * 3,
        out_specs=(hbm,) * 3,
        scratch_shapes=[dma((12,))],
        compiler_params=pltpu.CompilerParams(vmem_limit_bytes=1024 * 1024),
        name="put_out",
    )(*served)
    return down, scale, router.T


def solution(mesh):
    return jax.shard_map(
        body,
        mesh=mesh,
        in_specs=(P("ep", None, "fsdp"), P("fsdp", "ep"), P("fsdp")),
        out_specs=(P("ep", "fsdp", None), P("ep", "fsdp"), P()),
        check_vma=False,
    )
```

time: 178 us -> 94.6 us (0.53)
  the two profiles are of different devices: /device:TPU:8 before, /device:TPU:32 now
where the time goes in v2:
time: 94.6 us; the launch traced here: 93 us
  Pallas kernels  92.3 us (98%)
    pallas_call x1, Pallas kernels, body(): pl.pallas_call(serve, out_shape=outs, in_specs=[hbm] * 3, out_specs=(vmem...  90.5 us

profile of v2, /device:TPU:32, one launch (start us, length us, event | category | flops | bytes accessed | tf_op | source)
XLA Modules:
  0.0 93.0 jit_solution(10382543141454140106)
XLA Ops:
  0.6 90.5 %serve.1 = (bf16[2,200,4096]{2,1,0:T(8,128)(2,1)S(1)}, f32[2,200]{1,0:T(2,128)S(1)}, bf16[16,4096]{1,0:T(8,128)(2,1)S(1)}) custom-call(f32[2,6400,128]{2,1,0:T(8,128)} %w_ref.1, f32[2,128]{1,0:T(2,128)} %bitcast.3, f32[1,128]{1,0:T(1,128)} %bitcast.4), custom_call_target="tpu_custom_call" | custom-call | tf_op jit(solution)/shard_map/serve/pallas_call | solution.py:201
  91.1 1.8 %put_out.1 = (bf16[2,200,4096]{2,1,0:T(8,128)(2,1)}, f32[2,200]{1,0:T(2,128)}, bf16[16,4096]{1,0:T(8,128)(2,1)}) custom-call(bf16[2,200,4096]{2,1,0:T(8,128)(2,1)S(1)} %get-tuple-element.9.down_ref, f32[2,200]{1,0:T(2,128)S(1)} %get-tuple-element.10.scale_ref, bf16[16,4096]{1,0:T(8,128)(2,1)S(1)} %get-tuple-element.11.router_ref), custom_call_target="tpu_custom_call" | custom-call | tf_op jit(solution)/shard_map/put_out/pallas_call | solution.py:224

commit v3 on v2

v3 whole, which is shorter than its diff:
```python
import jax
import jax.numpy as jnp
from jax import lax
from jax.experimental import pallas as pl
from jax.experimental.pallas import tpu as pltpu
from jax.sharding import PartitionSpec as P

MESH = pl.DeviceIdType.MESH
F32, BF16 = jnp.float32, jnp.bfloat16
Z, X, EP = 8, 4, 8
PARTNERS = Z * X
ROWS = 200
CHUNKS = 4
FIRST = 2
VMEM_LIMIT = 40_000_000
PRE = tuple((4, dx) for dx in range(X))
R = 24


NEAR = sorted(
    ((dz, dx) for dz in range(Z) for dx in range(X) if dz or dx),
    key=lambda o: (min(o[0], Z - o[0]) + min(o[1], X - o[1]), o),
)
ORDER = (
    [(dz, dx) for dx in range(X) for dz in (1, 7)]
    + [(0, dx) for dx in (1, 2, 3)]
    + [(4, dx) for dx in (2, 1, 3, 0)]
    + [(dz, dx) for dx in (2, 1, 3, 0) for dz in (3, 5, 2, 6)]
)


def row_sums(block):
    square = block * block
    total = jnp.broadcast_to(jnp.sum(square, axis=1, keepdims=True), square.shape)
    rows = lax.broadcasted_iota(jnp.int32, (128, 128), 0)
    own = rows == lax.broadcasted_iota(jnp.int32, (128, 128), 1)
    return jnp.concatenate(
        [
            jnp.sum(
                jnp.where(own[: min(128, 2 * ROWS - r)], total[r : r + 128], 0.0),
                axis=0,
                keepdims=True,
            )
            for r in range(0, 2 * ROWS, 128)
        ],
        axis=1,
    )


def serve(
    w_ref, weight_ref, gain_ref, down_ref, scale_ref, router_ref,
    w, weight, gain, part, landed, total, scales, early, send, product, rows, columns,
    load_sem, part_send, part_recv, scale_send, scale_recv,
    early_send, early_recv, down_send, down_recv, router_send, router_recv, product_send, product_recv,
):
    ep, me = lax.axis_index("ep"), lax.axis_index("fsdp")
    z, x = me // X, lax.rem(me, X)

    each = PARTNERS // CHUNKS
    loads = []
    for c in range(CHUNKS):
        piece = pl.ds(c * each * ROWS, each * ROWS)
        loads.append((w_ref.at[:, piece, :], w.at[:, piece, :]))
    loads += [(weight_ref, weight), (gain_ref, gain)]
    loads = [pltpu.make_async_copy(*pair, load_sem.at[i]) for i, pair in enumerate(loads)]
    for load in loads[:FIRST] + loads[CHUNKS:]:
        load.start(priority=0)
    for load in loads[FIRST:CHUNKS]:
        load.start(priority=1)

    barrier = pltpu.get_barrier_semaphore()
    zs = [lax.rem(z + d, Z) * X for d in range(Z)]
    xs = [lax.rem(x + d, X) for d in range(X)]
    partners = [zs[dz] + xs[dx] for dz, dx in NEAR]
    peers = [lax.rem(ep + d, EP) for d in range(1, EP)]
    for t in reversed(partners):
        pl.semaphore_signal(barrier, inc=1, device_id={"fsdp": t}, device_id_type=MESH)
    for e in peers:
        pl.semaphore_signal(barrier, inc=1, device_id={"ep": e}, device_id_type=MESH)

    loads[CHUNKS].wait()
    loads[CHUNKS + 1].wait()
    product[...] = (weight[...] * gain[...]).astype(BF16)

    def rows_of(t):
        block = w[:, pl.ds(pl.multiple_of(t * ROWS, 8), ROWS), :]
        return block.reshape(2 * ROWS, 128)

    for c in range(CHUNKS):
        loads[c].wait()

        @pl.loop(c * each, (c + 1) * each, unroll=each)
        def _(t):
            part[t] = row_sums(rows_of(t))

    pl.semaphore_wait(barrier, len(partners) + len(peers))
    for t in reversed(partners):
        pltpu.make_async_remote_copy(
            src_ref=part.at[t], dst_ref=landed.at[me], send_sem=part_send, recv_sem=part_recv,
            device_id={"fsdp": t}, device_id_type=MESH,
        ).start()

    for i, (dz, dx) in enumerate(PRE):
        t = zs[dz] + xs[dx]
        pltpu.make_async_remote_copy(
            src_ref=w.at[:, pl.ds(pl.multiple_of(t * ROWS, 8), R), :], dst_ref=early.at[i], send_sem=early_send, recv_sem=early_recv,
            device_id={"fsdp": t}, device_id_type=MESH,
        ).start()

    landed[me] = part[me]
    others = pl.ds(0, PARTNERS - 1)
    pltpu.make_async_copy(landed.at[others], landed.at[others], part_recv).wait()
    scale = jnp.sqrt(jnp.sum(landed[...], axis=0))
    total[...] = scale
    scales[me] = scale
    for e in range(2):
        scale_ref[e : e + 1] = scale[:, e * ROWS : (e + 1) * ROWS]
    for t in partners:
        pltpu.make_async_remote_copy(
            src_ref=total, dst_ref=scales.at[me], send_sem=scale_send, recv_sem=scale_recv.at[me],
            device_id={"fsdp": t}, device_id_type=MESH,
        ).start()

    lanes = pl.ds(pl.multiple_of(me * 128, 128), 128)
    rows[:, lanes] = product[...]
    for t in partners:
        pltpu.make_async_remote_copy(
            src_ref=product, dst_ref=rows.at[:, lanes], send_sem=product_send, recv_sem=product_recv,
            device_id={"fsdp": t}, device_id_type=MESH,
        ).start()

    def scaled(t):
        inverse = 1.0 / scales[t, :, 0 : 2 * ROWS]
        return (rows_of(t) * jnp.broadcast_to(inverse, (128, 2 * ROWS)).T).astype(BF16)

    def make(t, first):
        pltpu.make_async_copy(scales.at[t], scales.at[t], scale_recv.at[t]).wait()
        value = scaled(t)
        send[t, 0, first:] = value[first:ROWS]
        send[t, 1, first:] = value[ROWS + first:]

    def go(t, first):
        left, kind = pl.ds(first, ROWS - first), int(first > 0)
        pltpu.make_async_remote_copy(
            src_ref=send.at[t, :, left], dst_ref=down_ref.at[:, left, lanes], send_sem=down_send.at[kind], recv_sem=down_recv.at[kind],
            device_id={"fsdp": t}, device_id_type=MESH,
        ).start()

    last = None
    for o in ORDER:
        this = zs[o[0]] + xs[o[1]], R if o in PRE else 0
        make(*this)
        if last is not None:
            go(*last)
        last = this
    go(*last)

    some = rows.at[:, pl.ds(0, (PARTNERS - 1) * 128)]
    pltpu.make_async_copy(some, some, product_recv).wait()
    columns[ep] = rows[...]
    for e in peers:
        pltpu.make_async_remote_copy(
            src_ref=rows, dst_ref=columns.at[ep], send_sem=router_send, recv_sem=router_recv,
            device_id={"ep": e}, device_id_type=MESH,
        ).start()
    pltpu.make_async_copy(some, some, product_send).wait()

    few = early.at[pl.ds(0, len(PRE))]
    pltpu.make_async_copy(few, few, early_recv).wait()
    inverse = jnp.broadcast_to(1.0 / scale[:, 0:400], (128, 400)).T
    for i, (dz, dx) in enumerate(PRE):
        s = zs[(8 - dz) % 8] + xs[(4 - dx) % 4]
        for e in range(2):
            down_ref[e, 0:R, pl.ds(pl.multiple_of(s * 128, 128), 128)] = (early[i, e] * inverse[e * ROWS : e * ROWS + R]).astype(BF16)
    pltpu.make_async_copy(few, few, early_send).wait()

    own = scaled(me)
    down_ref[0, :, lanes] = own[:ROWS]
    down_ref[1, :, lanes] = own[ROWS:]

    pltpu.make_async_copy(columns.at[pl.ds(0, EP - 1)], columns.at[pl.ds(0, EP - 1)], router_recv).wait()
    for e in range(EP):
        router_ref[2 * e : 2 * e + 2, :] = columns[e]

    pltpu.make_async_copy(part.at[others], part.at[others], part_send).wait()
    pltpu.make_async_copy(scales.at[others], scales.at[others], scale_send).wait()
    pltpu.make_async_copy(columns.at[pl.ds(0, EP - 1)], columns.at[pl.ds(0, EP - 1)], router_send).wait()
    for sem in (down_send, down_recv):
        k = PARTNERS - 1 - len(PRE)
        pltpu.make_async_copy(send.at[pl.ds(0, k)], send.at[pl.ds(0, k)], sem.at[0]).wait()
        p = send.at[pl.ds(0, len(PRE)), :, pl.ds(R, ROWS - R)]
        pltpu.make_async_copy(p, p, sem.at[1]).wait()


def put_out(down_ref, scale_ref, router_ref, down_out, scale_out, router_out, sem):
    pairs = [(scale_ref, scale_out), (router_ref, router_out)]
    for e in range(2):
        pairs.append((down_ref.at[e], down_out.at[e]))
    copies = [pltpu.make_async_copy(*pair, sem.at[i]) for i, pair in enumerate(pairs)]
    for copy in copies:
        copy.start()
    for copy in copies:
        copy.wait()


def body(w_down, router_weight, router_gain):
    vmem, hbm = pl.BlockSpec(memory_space=pltpu.VMEM), pl.BlockSpec(memory_space=pltpu.HBM)
    dma = pltpu.SemaphoreType.DMA
    outs = (
        jax.ShapeDtypeStruct((2, ROWS, PARTNERS * 128), BF16),
        jax.ShapeDtypeStruct((2, ROWS), F32),
        jax.ShapeDtypeStruct((2 * EP, PARTNERS * 128), BF16),
    )
    operands = (w_down, router_weight.T, router_gain[None])
    served = pl.pallas_call(
        serve,
        out_shape=outs,
        in_specs=[hbm] * 3,
        out_specs=(vmem,) * 3,
        scratch_shapes=[
            pltpu.VMEM((2, PARTNERS * ROWS, 128), F32),
            pltpu.VMEM((2, 128), F32),
            pltpu.VMEM((1, 128), F32),
            pltpu.VMEM((PARTNERS, 1, 512), F32),
            pltpu.VMEM((PARTNERS, 1, 512), F32),
            pltpu.VMEM((1, 512), F32),
            pltpu.VMEM((PARTNERS, 1, 512), F32),
            pltpu.VMEM((len(PRE), 2, R, 128), F32),
            pltpu.VMEM((PARTNERS, 2, ROWS, 128), BF16),
            pltpu.VMEM((2, 128), BF16),
            pltpu.VMEM((2, PARTNERS * 128), BF16),
            pltpu.VMEM((EP, 2, PARTNERS * 128), BF16),
            dma((CHUNKS + 2,)), dma, dma, dma, dma((PARTNERS,)), dma, dma, dma((2,)), dma((2,)), dma, dma, dma, dma,
        ],
        compiler_params=pltpu.CompilerParams(
            collective_id=0, has_side_effects=True, vmem_limit_bytes=VMEM_LIMIT
        ),
        name="serve",
    )(*(pltpu.with_memory_space_constraint(a, pltpu.HBM) for a in operands))
    down, scale, router = pl.pallas_call(
        put_out,
        out_shape=outs,
        in_specs=[vmem] * 3,
        out_specs=(hbm,) * 3,
        scratch_shapes=[dma((4,))],
        compiler_params=pltpu.CompilerParams(vmem_limit_bytes=1024 * 1024),
        name="put_out",
    )(*served)
    return down, scale, router.T


def solution(mesh):
    return jax.shard_map(
        body,
        mesh=mesh,
        in_specs=(P("ep", None, "fsdp"), P("fsdp", "ep"), P("fsdp")),
        out_specs=(P("ep", "fsdp", None), P("ep", "fsdp"), P()),
        check_vma=False,
    )
```

time: 94.6 us -> 91.3 us (0.965); the launches traced: 93 us -> 91.3 us
  Pallas kernels: 92.3 us -> 90.6 us
    pallas_call x1, Pallas kernels: 90.5 us -> 88.8 us  [body(): pl.pallas_call(serve, out_shape=outs, in_specs=[hbm] * 3, out_specs=(vmem...]
where the time goes in v3:
time: 91.3 us
  Pallas kernels  90.6 us (99%)
    pallas_call x1, Pallas kernels, body(): pl.pallas_call(serve, out_shape=outs, in_specs=[hbm] * 3, out_specs=(vmem...  88.8 us

profile of v3, /device:TPU:32, one launch (start us, length us, event | category | flops | bytes accessed | tf_op | source)
XLA Modules:
  0.0 91.3 jit_solution(1255029989224877986)
XLA Ops:
  0.6 88.8 %serve.1 = (bf16[2,200,4096]{2,1,0:T(8,128)(2,1)S(1)}, f32[2,200]{1,0:T(2,128)S(1)}, bf16[16,4096]{1,0:T(8,128)(2,1)S(1)}) custom-call(f32[2,6400,128]{2,1,0:T(8,128)} %w_ref.1, f32[2,128]{1,0:T(2,128)} %bitcast.3, f32[1,128]{1,0:T(1,128)} %bitcast.4), custom_call_target="tpu_custom_call" | custom-call | tf_op jit(solution)/shard_map/serve/pallas_call | solution.py:215
  89.5 1.8 %put_out.1 = (bf16[2,200,4096]{2,1,0:T(8,128)(2,1)}, f32[2,200]{1,0:T(2,128)}, bf16[16,4096]{1,0:T(8,128)(2,1)}) custom-call(bf16[2,200,4096]{2,1,0:T(8,128)(2,1)S(1)} %get-tuple-element.9.down_ref, f32[2,200]{1,0:T(2,128)S(1)} %get-tuple-element.10.scale_ref, bf16[16,4096]{1,0:T(8,128)(2,1)S(1)} %get-tuple-element.11.router_ref), custom_call_target="tpu_custom_call" | custom-call | tf_op jit(solution)/shard_map/put_out/pallas_call | solution.py:240

commit v4 on v3

--- a/solution.py
+++ b/solution.py
@@ -63,10 +63,8 @@
         loads.append((w_ref.at[:, piece, :], w.at[:, piece, :]))
     loads += [(weight_ref, weight), (gain_ref, gain)]
     loads = [pltpu.make_async_copy(*pair, load_sem.at[i]) for i, pair in enumerate(loads)]
-    for load in loads[:FIRST] + loads[CHUNKS:]:
+    for load in loads[:FIRST]:
         load.start(priority=0)
-    for load in loads[FIRST:CHUNKS]:
-        load.start(priority=1)
 
     barrier = pltpu.get_barrier_semaphore()
     zs = [lax.rem(z + d, Z) * X for d in range(Z)]
@@ -78,36 +76,41 @@
     for e in peers:
         pl.semaphore_signal(barrier, inc=1, device_id={"ep": e}, device_id_type=MESH)
 
+    for load in loads[FIRST:CHUNKS]:
+        load.start(priority=1)
+    for load in loads[CHUNKS:]:
+        load.start()
+
+
+    def rows_of(t):
+        block = w[:, pl.ds(pl.multiple_of(t * ROWS, 8), ROWS), :]
+        return block.reshape(2 * ROWS, 128)
+
+    for c in range(CHUNKS):
+        loads[c].wait()
+
+        @pl.loop(c * each, (c + 1) * each, unroll=each)
+        def _(t):
+            part[t] = row_sums(rows_of(t))
+
+    pl.semaphore_wait(barrier, len(partners) + len(peers))
+    for t in reversed(partners):
+        pltpu.make_async_remote_copy(
+            src_ref=part.at[t], dst_ref=landed.at[me], send_sem=part_send, recv_sem=part_recv,
+            device_id={"fsdp": t}, device_id_type=MESH,
+        ).start()
+
+    for i, (dz, dx) in enumerate(PRE):
+        t = zs[dz] + xs[dx]
+        pltpu.make_async_remote_copy(
+            src_ref=w.at[:, pl.ds(pl.multiple_of(t * ROWS, 8), R), :], dst_ref=early.at[i], send_sem=early_send, recv_sem=early_recv,
+            device_id={"fsdp": t}, device_id_type=MESH,
+        ).start()
+
+    landed[me] = part[me]
     loads[CHUNKS].wait()
     loads[CHUNKS + 1].wait()
     product[...] = (weight[...] * gain[...]).astype(BF16)
-
-    def rows_of(t):
-        block = w[:, pl.ds(pl.multiple_of(t * ROWS, 8), ROWS), :]
-        return block.reshape(2 * ROWS, 128)
-
-    for c in range(CHUNKS):
-        loads[c].wait()
-
-        @pl.loop(c * each, (c + 1) * each, unroll=each)
-        def _(t):
-            part[t] = row_sums(rows_of(t))
-
-    pl.semaphore_wait(barrier, len(partners) + len(peers))
-    for t in reversed(partners):
-        pltpu.make_async_remote_copy(
-            src_ref=part.at[t], dst_ref=landed.at[me], send_sem=part_send, recv_sem=part_recv,
-            device_id={"fsdp": t}, device_id_type=MESH,
-        ).start()
-
-    for i, (dz, dx) in enumerate(PRE):
-        t = zs[dz] + xs[dx]
-        pltpu.make_async_remote_copy(
-            src_ref=w.at[:, pl.ds(pl.multiple_of(t * ROWS, 8), R), :], dst_ref=early.at[i], send_sem=early_send, recv_sem=early_recv,
-            device_id={"fsdp": t}, device_id_type=MESH,
-        ).start()
-
-    landed[me] = part[me]
     others = pl.ds(0, PARTNERS - 1)
     pltpu.make_async_copy(landed.at[others], landed.at[others], part_recv).wait()
     scale = jnp.sqrt(jnp.sum(landed[...], axis=0))
@@ -197,7 +200,7 @@
     for e in range(2):
         pairs.append((down_ref.at[e], down_out.at[e]))
     copies = [pltpu.make_async_copy(*pair, sem.at[i]) for i, pair in enumerate(pairs)]
-    for copy in copies:
+    for copy in reversed(copies):
         copy.start()
     for copy in copies:
         copy.wait()

time: 91.3 us -> 91.3 us (level)
  no operation moved by 1% of the time
where the time goes in v4:
time: 91.3 us
  Pallas kernels  90.6 us (99%)
    pallas_call x1, Pallas kernels, body(): pl.pallas_call(serve, out_shape=outs, in_specs=[hbm] * 3, out_specs=(vmem...  88.8 us

profile of v4, /device:TPU:32, one launch (start us, length us, event | category | flops | bytes accessed | tf_op | source)
XLA Modules:
  0.0 91.3 jit_solution(6976080320945962534)
XLA Ops:
  0.6 88.8 %serve.1 = (bf16[2,200,4096]{2,1,0:T(8,128)(2,1)S(1)}, f32[2,200]{1,0:T(2,128)S(1)}, bf16[16,4096]{1,0:T(8,128)(2,1)S(1)}) custom-call(f32[2,6400,128]{2,1,0:T(8,128)} %w_ref.1, f32[2,128]{1,0:T(2,128)} %bitcast.3, f32[1,128]{1,0:T(1,128)} %bitcast.4), custom_call_target="tpu_custom_call" | custom-call | tf_op jit(solution)/shard_map/serve/pallas_call | solution.py:218
  89.5 1.8 %put_out.1 = (bf16[2,200,4096]{2,1,0:T(8,128)(2,1)}, f32[2,200]{1,0:T(2,128)}, bf16[16,4096]{1,0:T(8,128)(2,1)}) custom-call(bf16[2,200,4096]{2,1,0:T(8,128)(2,1)S(1)} %get-tuple-element.9.down_ref, f32[2,200]{1,0:T(2,128)S(1)} %get-tuple-element.10.scale_ref, bf16[16,4096]{1,0:T(8,128)(2,1)S(1)} %get-tuple-element.11.router_ref), custom_call_target="tpu_custom_call" | custom-call | tf_op jit(solution)/shard_map/put_out/pallas_call | solution.py:243
